TPU v7x, 32 devices: a whole 2x2x4 slice. The times are simulated.
32 devices in a mesh: section: 4 (over z), dp: 2 (over y), tensor: 4 (over x, core).
Axes of the slice: x: 2, y: 2, z: 4, core: 2. Of those that a mesh axis runs over, the one named last changes fastest.
Arguments:
- inputs: bfloat16 [8, 2, 64, 2560], P('dp', None, None, ('section', 'tensor')), parts along dimension 0, may hold values from -18 to 18
- sequence_jobs: int32 [8, 2, 1], P('dp'), parts along dimension 0, may hold values from 0 to 3
- entry_sequence: int32 [8], P('dp'), parts along dimension 0, may hold values from 0 to 3, each once
- layer_norm_gain: float32 [4, 2560], P('section'), may hold values from 0.25 to 1.75
- frozen_query_matrix: bfloat16 [4, 2560, 2560], P('section', None, 'tensor'), may hold values from -1 to 1
- frozen_key_matrix: bfloat16 [4, 2560, 2560], P('section', None, 'tensor'), may hold values from -24 to 24
- frozen_value_matrix: bfloat16 [4, 2560, 2560], P('section', None, 'tensor'), may hold values from -0.125 to 0.125
- frozen_output_matrix: bfloat16 [4, 2560, 2560], P('section', 'tensor'), may hold values from -0.125 to 0.125
- adapter_down_maps: bfloat16 [4, 2560, 128], P('section', 'tensor'), may hold values from -0.125 to 0.125
- adapter_up_maps: bfloat16 [4, 2, 64, 2560], P('section', None, None, 'tensor'), may hold values from -1.5 to 1.5
Outputs:
- finished: bfloat16 [8, 2, 64, 2560], P('dp', None, None, ('section', 'tensor')), parts along dimension 0
There are 2 independent parts, one for each index of `dp`. A program takes and returns all parts, laid end to end along the dimension named above; an argument that names none is the same for every part. Nothing has to cross between parts.
Inputs may be any that keep to these rules, and one draw needn't show every extreme that they name: `sequence_jobs`: every one of the 4 jobs owns at least one sequence. `entry_sequence`: a permutation of the 4 micro-batches.
All inputs are finite; a program needn't handle non-finite values.
Results may differ from a plain program's by a relative error of at most 0.039.
Values may be sent and summed in bfloat16 or wider, within the bound.
A program may use at most 64 MiB of HBM per device.

v0:
```python
import jax
import jax.numpy as jnp
from jax import lax
from jax.sharding import PartitionSpec as P

HEAD_DIM = 128
ADAPTER_RANK = 16
ADAPTER_JOBS = 4
adapter_scale = 2.0


def shifted(value, axis, steps):
    count = lax.axis_size(axis)
    leading, last = (max(0, -steps), min(count, count - steps))
    return lax.ppermute(value, axis, [(source, source + steps) for source in range(leading, last)])


def spread(array, axis, root):
    mine = lax.axis_index(axis) == root
    return lax.psum(jnp.where(mine, array, jnp.zeros_like(array)), axis)


def attend(query_rows, key_vecs, value_rows, head_groupings, sequence_length):
    head_count = query_rows.shape[1] // HEAD_DIM
    grid_shape = (head_groupings, sequence_length, head_count, HEAD_DIM)
    scores = jnp.einsum(
        "bqhd,bkhd->bhqk",
        query_rows.reshape(grid_shape),
        key_vecs.reshape(grid_shape),
        preferred_element_type=jnp.float32,
    ) * HEAD_DIM ** (-0.5)
    causal = lax.broadcasted_iota(
        jnp.int32, (sequence_length, sequence_length), 0
    ) >= lax.broadcasted_iota(jnp.int32, (sequence_length, sequence_length), 1)
    scores = jnp.where(causal, scores, -jnp.inf)
    row_max = jnp.max(scores, axis=-1, keepdims=True)
    weights = jnp.exp(scores - row_max)
    probabilities = (weights / jnp.sum(weights, axis=-1, keepdims=True)).astype(jnp.bfloat16)
    mixture = jnp.einsum(
        "bhqk,bkhd->bqhd",
        probabilities,
        value_rows.reshape(grid_shape),
        preferred_element_type=jnp.float32,
    )
    return mixture.astype(jnp.bfloat16).reshape(
        head_groupings * sequence_length, head_count * HEAD_DIM
    )


def prepare_inputs(
    complete_result, inverse_norm_scale, adapter_rows, partition_number, column_slice
):
    widened = complete_result.astype(jnp.float32)
    meansq = jnp.mean(widened * widened, axis=-1, keepdims=True)
    normalized_input = (widened * lax.rsqrt(meansq + 1e-05) * inverse_norm_scale).astype(
        jnp.bfloat16
    )
    local_normalized = lax.dynamic_slice_in_dim(
        normalized_input, partition_number * column_slice, column_slice, 1
    )
    return (
        normalized_input,
        jnp.dot(local_normalized, adapter_rows, preferred_element_type=jnp.float32),
    )


def final_output(
    normalized_input,
    lowrank_products,
    query_matrix,
    key_matrix,
    value_matrix,
    output_matrix,
    adapter_upper_part,
    head_groupings,
    sequence_length,
):
    middle_result = lowrank_products.shape[1] // 2
    query_rows = (
        jnp.dot(normalized_input, query_matrix, preferred_element_type=jnp.float32)
        + adapter_scale
        * jnp.dot(
            lowrank_products[:, :middle_result],
            adapter_upper_part[0],
            preferred_element_type=jnp.float32,
        )
    ).astype(jnp.bfloat16)
    key_vecs = jnp.dot(normalized_input, key_matrix, preferred_element_type=jnp.float32).astype(
        jnp.bfloat16
    )
    value_rows = (
        jnp.dot(normalized_input, value_matrix, preferred_element_type=jnp.float32)
        + adapter_scale
        * jnp.dot(
            lowrank_products[:, middle_result:],
            adapter_upper_part[1],
            preferred_element_type=jnp.float32,
        )
    ).astype(jnp.bfloat16)
    heads = attend(query_rows, key_vecs, value_rows, head_groupings, sequence_length)
    return (
        jnp.dot(heads, output_matrix, preferred_element_type=jnp.float32)
        .astype(jnp.bfloat16)
        .astype(jnp.float32)
    )


def shards(
    inputs,
    sequence_jobs,
    entry_sequence,
    layer_norm_gain,
    frozen_query_matrix,
    frozen_key_matrix,
    frozen_value_matrix,
    frozen_output_matrix,
    adapter_down_maps,
    adapter_up_maps,
):
    sections = lax.axis_size("section")
    across = lax.axis_size("tensor")
    section_id = lax.axis_index("section")
    partition_number = lax.axis_index("tensor")
    entire = lax.all_gather(inputs, ("section", "tensor"), axis=3, tiled=True)
    batches, head_groupings, sequence_length, features = entire.shape
    column_slice = frozen_query_matrix.shape[2]
    lowrank_width = adapter_down_maps.shape[2]
    tok_rows = head_groupings * sequence_length
    step_count = batches + sections - 1

    def compute(complete_result, step_idx):
        position = step_idx - section_id
        active = jnp.logical_and(position >= 0, position < batches)
        chosen = entry_sequence[jnp.clip(position, 0, batches - 1)]
        seq_jobs = lax.dynamic_index_in_dim(sequence_jobs, chosen, 0, keepdims=False)
        job_per_row = jnp.repeat(seq_jobs[:, 0], sequence_length)
        normalized_input, part_codes = lax.cond(
            active,
            lambda: prepare_inputs(
                complete_result,
                layer_norm_gain[0],
                adapter_down_maps[0],
                partition_number,
                column_slice,
            ),
            lambda: (
                jnp.zeros((tok_rows, features), jnp.bfloat16),
                jnp.zeros((tok_rows, lowrank_width), jnp.float32),
            ),
        )
        summed_codes = lax.psum(part_codes, "tensor")
        column_job = (
            lax.broadcasted_iota(jnp.int32, (lowrank_width,), 0) // ADAPTER_RANK % ADAPTER_JOBS
        )
        lowrank_products = jnp.where(
            column_job[None, :] == job_per_row[:, None], summed_codes, 0.0
        ).astype(jnp.bfloat16)
        return lax.cond(
            active,
            lambda: final_output(
                normalized_input,
                lowrank_products,
                frozen_query_matrix[0],
                frozen_key_matrix[0],
                frozen_value_matrix[0],
                frozen_output_matrix[0],
                adapter_up_maps[0],
                head_groupings,
                sequence_length,
            ),
            lambda: jnp.zeros((tok_rows, features), jnp.float32),
        )

    def injected(step_idx):
        chosen = entry_sequence[jnp.minimum(step_idx, batches - 1)]
        return lax.dynamic_index_in_dim(entire, chosen, 0, keepdims=False).reshape(
            tok_rows, features
        )

    def record(stored, step_idx, piece):
        out_slot = step_idx - (sections - 1)
        keeping = jnp.logical_and(section_id == sections - 1, out_slot >= 0)
        updated = lax.dynamic_update_index_in_dim(stored, piece, jnp.maximum(out_slot, 0), 0)
        return jnp.where(keeping, updated, stored)

    stored = jnp.zeros((batches, tok_rows, column_slice), jnp.bfloat16)

    def advance(step_idx, carried):
        arrived, stored = carried
        entering = lax.dynamic_slice_in_dim(
            injected(step_idx), partition_number * column_slice, column_slice, 1
        )
        owned = jnp.where(section_id == 0, entering, arrived)
        complete_result = lax.all_gather(owned, "tensor", axis=1, tiled=True)
        term = compute(complete_result, step_idx)
        share = lax.psum_scatter(
            term.astype(jnp.bfloat16), "tensor", scatter_dimension=1, tiled=True
        ).astype(jnp.float32)
        updated_x = (owned.astype(jnp.float32) + share).astype(jnp.bfloat16)
        stored = record(stored, step_idx, updated_x)
        arrived = shifted(updated_x, ("section", "tensor"), across)
        return (arrived, stored)

    initial = jnp.zeros((tok_rows, column_slice), jnp.bfloat16)
    arrived, stored = lax.fori_loop(0, step_count, advance, (initial, stored))
    result = spread(stored, "section", sections - 1)
    complete = lax.all_gather(result, "tensor", axis=2, tiled=True)
    width = features // (sections * across)
    piece = lax.dynamic_slice_in_dim(
        complete, (section_id * across + partition_number) * width, width, 2
    )
    return piece.reshape(batches, head_groupings, sequence_length, width)


def solution(mesh):
    in_specs = (
        P("dp", None, None, ("section", "tensor")),
        P("dp", None, None),
        P("dp"),
        P("section", None),
        P("section", None, "tensor"),
        P("section", None, "tensor"),
        P("section", None, "tensor"),
        P("section", "tensor", None),
        P("section", "tensor", None),
        P("section", None, None, "tensor"),
    )
    out_specs = P("dp", None, None, ("section", "tensor"))
    return jax.shard_map(shards, mesh=mesh, in_specs=in_specs, out_specs=out_specs, check_vma=False)
```

profile of v0, /device:TPU:0, one launch (start us, length us, event | category | flops | bytes accessed | tf_op | source)
XLA Modules:
  0.0 737.4 jit_solution(598932090509238109)
XLA Ops:
  9.2 58.9 %all-gather.3.cloned.1.call-done = bf16[4,2,64,2560]{2,0,1,3:T(4,128)(2,1)} async-done(((bf16[4,2,64,160]{2,0,1,3:T(4,128)(2,1)}), bf16[4,2,64,2560]{2,0,1,3:T(4,128)(2,1)}) %all-gather.3.cloned.1.call-update) | async-done | bytes 2621456 | tf_op jit(solution)/shard_map/all_gather | solution.py:124
  68.1 8.5 %copy.28 = bf16[4,2,64,2560]{3,2,1,0:T(8,128)(2,1)} copy(bf16[4,2,64,2560]{2,0,1,3:T(4,128)(2,1)} %all-gather.3.cloned.1.call-done) | data formatting | bytes 5242880 | tf_op jit(solution)/shard_map/while | solution.py:205
  77.5 579.8 %while.17 = (s32[]{:T(128)}, bf16[128,640]{1,0:T(8,128)(2,1)S(1)}, bf16[4,128,640]{2,1,0:T(8,128)(2,1)}, pred[]{:T(512)}, s32[4]{0:T(128)S(1)}, /*index=5*/bf16[...) while((s32[]{:T(128)}, bf16[128,640]{1,0:T(8,128)(2,1)S(1)}, ...), condition=%wide.region_10.11_spmd, body=%wide.region_0.10_spmd.sunk | while | flops 1744747648 | bytes 44909328 | solution.py:205
  82.6 7.9 %all_gather.19 = bf16[128,2560]{1,0:T(8,128)(2,1)S(1)} all-gather(bf16[128,640]{1,0:T(8,128)(2,1)S(1)} %dynamic-slice_select_fusion.2), channel_id=1, replica_groups=mesh['section'=4,'dp'=2,'tensor'=4] {'tensor'}, dimensions={1}, use_global_device_ids=true | all-gather | bytes 819200 | tf_op jit(solution)/shard_map/while/body/eval_jaxpr/all_gather | solution.py:194
  93.0 11.1 %psum.23 = bf16[128,128]{1,0:T(8,128)(2,1)S(1)} all-reduce(f32[128,128]{1,0:T(8,128)S(1)} %get-tuple-element.638), channel_id=1, replica_groups=mesh['section'=4,'dp'=2,'tensor'=4] {'tensor'}, use_global_device_ids=true, to_apply=%region_4.4 | all-reduce | flops 16384 | bytes 98304 | tf_op jit(solution)/shard_map/while/body/eval_jaxpr/psum | solution.py:151
  105.1 22.0 %conditional.5 = (bf16[128,2560]{1,0:T(8,128)(2,1)S(1)}) conditional(s32[]{:T(128)} %convert_element_type.120, () %tuple.63, (bf16[1,2560,640]{2,1,0:T(8,128)(2,1)}, bf16[128,2560]{1,0:T(8,128)(2,1)}, bf16[128,128]{1,0:T(8,128)(2,1)S(1)}, bf16[1,2,64,640]{3,2,1,0:T(8,128)(2,1)}, bf16[1,2560,640]{2,1,0:T(8,128)(2,1)}, ...), branch_computations={%region_5.5_spmd, %region_6.8_spmd} | conditional | flops 1720939136 | bytes 34157632 | solution.py:158
  128.3 20.7 %reduce-scatter.6.cloned.1.call-done = bf16[640,128]{1,0:T(8,128)(2,1)} async-done(((bf16[2560,128]{1,0:T(8,128)(2,1)}), bf16[640,128]{1,0:T(8,128)(2,1)}) %reduce-scatter.6.cloned.1.call-update) | async-done | bytes 163856 | tf_op jit(solution)/shard_map/while
  172.9 12.0 %psum.23 = bf16[128,128]{1,0:T(8,128)(2,1)S(1)} all-reduce(f32[128,128]{1,0:T(8,128)S(1)} %get-tuple-element.638), channel_id=1, replica_groups=mesh['section'=4,'dp'=2,'tensor'=4] {'tensor'}, use_global_device_ids=true, to_apply=%region_4.4 | all-reduce | flops 16384 | bytes 98304 | tf_op jit(solution)/shard_map/while/body/eval_jaxpr/psum | solution.py:151
  185.8 22.1 %conditional.5 = (bf16[128,2560]{1,0:T(8,128)(2,1)S(1)}) conditional(s32[]{:T(128)} %convert_element_type.120, () %tuple.63, (bf16[1,2560,640]{2,1,0:T(8,128)(2,1)}, bf16[128,2560]{1,0:T(8,128)(2,1)}, bf16[128,128]{1,0:T(8,128)(2,1)S(1)}, bf16[1,2,64,640]{3,2,1,0:T(8,128)(2,1)}, bf16[1,2560,640]{2,1,0:T(8,128)(2,1)}, ...), branch_computations={%region_5.5_spmd, %region_6.8_spmd} | conditional | flops 1720939136 | bytes 34157632 | solution.py:158
  209.0 21.8 %reduce-scatter.6.cloned.1.call-done = bf16[640,128]{1,0:T(8,128)(2,1)} async-done(((bf16[2560,128]{1,0:T(8,128)(2,1)}), bf16[640,128]{1,0:T(8,128)(2,1)}) %reduce-scatter.6.cloned.1.call-update) | async-done | bytes 163856 | tf_op jit(solution)/shard_map/while
  254.7 12.0 %psum.23 = bf16[128,128]{1,0:T(8,128)(2,1)S(1)} all-reduce(f32[128,128]{1,0:T(8,128)S(1)} %get-tuple-element.638), channel_id=1, replica_groups=mesh['section'=4,'dp'=2,'tensor'=4] {'tensor'}, use_global_device_ids=true, to_apply=%region_4.4 | all-reduce | flops 16384 | bytes 98304 | tf_op jit(solution)/shard_map/while/body/eval_jaxpr/psum | solution.py:151
  267.6 22.1 %conditional.5 = (bf16[128,2560]{1,0:T(8,128)(2,1)S(1)}) conditional(s32[]{:T(128)} %convert_element_type.120, () %tuple.63, (bf16[1,2560,640]{2,1,0:T(8,128)(2,1)}, bf16[128,2560]{1,0:T(8,128)(2,1)}, bf16[128,128]{1,0:T(8,128)(2,1)S(1)}, bf16[1,2,64,640]{3,2,1,0:T(8,128)(2,1)}, bf16[1,2560,640]{2,1,0:T(8,128)(2,1)}, ...), branch_computations={%region_5.5_spmd, %region_6.8_spmd} | conditional | flops 1720939136 | bytes 34157632 | solution.py:158
  290.8 22.7 %reduce-scatter.6.cloned.1.call-done = bf16[640,128]{1,0:T(8,128)(2,1)} async-done(((bf16[2560,128]{1,0:T(8,128)(2,1)}), bf16[640,128]{1,0:T(8,128)(2,1)}) %reduce-scatter.6.cloned.1.call-update) | async-done | bytes 163856 | tf_op jit(solution)/shard_map/while
  337.4 12.0 %psum.23 = bf16[128,128]{1,0:T(8,128)(2,1)S(1)} all-reduce(f32[128,128]{1,0:T(8,128)S(1)} %get-tuple-element.638), channel_id=1, replica_groups=mesh['section'=4,'dp'=2,'tensor'=4] {'tensor'}, use_global_device_ids=true, to_apply=%region_4.4 | all-reduce | flops 16384 | bytes 98304 | tf_op jit(solution)/shard_map/while/body/eval_jaxpr/psum | solution.py:151
  350.3 22.1 %conditional.5 = (bf16[128,2560]{1,0:T(8,128)(2,1)S(1)}) conditional(s32[]{:T(128)} %convert_element_type.120, () %tuple.63, (bf16[1,2560,640]{2,1,0:T(8,128)(2,1)}, bf16[128,2560]{1,0:T(8,128)(2,1)}, bf16[128,128]{1,0:T(8,128)(2,1)S(1)}, bf16[1,2,64,640]{3,2,1,0:T(8,128)(2,1)}, bf16[1,2560,640]{2,1,0:T(8,128)(2,1)}, ...), branch_computations={%region_5.5_spmd, %region_6.8_spmd} | conditional | flops 1720939136 | bytes 34157632 | solution.py:158
  373.5 23.6 %reduce-scatter.6.cloned.1.call-done = bf16[640,128]{1,0:T(8,128)(2,1)} async-done(((bf16[2560,128]{1,0:T(8,128)(2,1)}), bf16[640,128]{1,0:T(8,128)(2,1)}) %reduce-scatter.6.cloned.1.call-update) | async-done | bytes 163856 | tf_op jit(solution)/shard_map/while
  419.3 12.0 %psum.23 = bf16[128,128]{1,0:T(8,128)(2,1)S(1)} all-reduce(f32[128,128]{1,0:T(8,128)S(1)} %get-tuple-element.638), channel_id=1, replica_groups=mesh['section'=4,'dp'=2,'tensor'=4] {'tensor'}, use_global_device_ids=true, to_apply=%region_4.4 | all-reduce | flops 16384 | bytes 98304 | tf_op jit(solution)/shard_map/while/body/eval_jaxpr/psum | solution.py:151
  433.5 47.2 %reduce-scatter.6.cloned.1.call-done = bf16[640,128]{1,0:T(8,128)(2,1)} async-done(((bf16[2560,128]{1,0:T(8,128)(2,1)}), bf16[640,128]{1,0:T(8,128)(2,1)}) %reduce-scatter.6.cloned.1.call-update) | async-done | bytes 163856 | tf_op jit(solution)/shard_map/while
  502.9 12.0 %psum.23 = bf16[128,128]{1,0:T(8,128)(2,1)S(1)} all-reduce(f32[128,128]{1,0:T(8,128)S(1)} %get-tuple-element.638), channel_id=1, replica_groups=mesh['section'=4,'dp'=2,'tensor'=4] {'tensor'}, use_global_device_ids=true, to_apply=%region_4.4 | all-reduce | flops 16384 | bytes 98304 | tf_op jit(solution)/shard_map/while/body/eval_jaxpr/psum | solution.py:151
  517.1 47.2 %reduce-scatter.6.cloned.1.call-done = bf16[640,128]{1,0:T(8,128)(2,1)} async-done(((bf16[2560,128]{1,0:T(8,128)(2,1)}), bf16[640,128]{1,0:T(8,128)(2,1)}) %reduce-scatter.6.cloned.1.call-update) | async-done | bytes 163856 | tf_op jit(solution)/shard_map/while
  586.5 12.0 %psum.23 = bf16[128,128]{1,0:T(8,128)(2,1)S(1)} all-reduce(f32[128,128]{1,0:T(8,128)S(1)} %get-tuple-element.638), channel_id=1, replica_groups=mesh['section'=4,'dp'=2,'tensor'=4] {'tensor'}, use_global_device_ids=true, to_apply=%region_4.4 | all-reduce | flops 16384 | bytes 98304 | tf_op jit(solution)/shard_map/while/body/eval_jaxpr/psum | solution.py:151
  600.7 47.2 %reduce-scatter.6.cloned.1.call-done = bf16[640,128]{1,0:T(8,128)(2,1)} async-done(((bf16[2560,128]{1,0:T(8,128)(2,1)}), bf16[640,128]{1,0:T(8,128)(2,1)}) %reduce-scatter.6.cloned.1.call-update) | async-done | bytes 163856 | tf_op jit(solution)/shard_map/while
  658.3 43.7 %all-reduce.2.cloned.1.call-done = bf16[4,128,640]{2,1,0:T(8,128)(2,1)} async-done(((bf16[4,128,640]{2,1,0:T(8,128)(2,1)}), bf16[4,128,640]{2,1,0:T(8,128)(2,1)}) %all-reduce.2.cloned.1.call-update) | async-done | bytes 655376 | tf_op jit(solution)/shard_map/psum | solution.py:20
  702.0 26.7 %all-gather.5.cloned.1.call-done = bf16[4,128,2560]{2,1,0:T(8,128)(2,1)} async-done(((bf16[4,128,640]{2,1,0:T(8,128)(2,1)}), bf16[4,128,2560]{2,1,0:T(8,128)(2,1)}) %all-gather.5.cloned.1.call-update) | async-done | bytes 2621456 | tf_op jit(solution)/shard_map/all_gather | solution.py:207
  (238 shorter events, 249.9 us)
Async XLA Ops:
  6.5 61.6 %all-gather.3.cloned.1.call-start = ((), (), s32[]{:S(2)}) async-start(), calls=%async_computation.1 | async-start | bytes 5570560 | tf_op jit(solution)/shard_map/all_gather | solution.py:124
  9.2 68.3 %copy-start.1 = (f32[1,2560]{1,0:T(1,128)S(1)}, f32[1,2560]{1,0:T(1,128)}, u32[]{:S(2)}) copy-start(f32[1,2560]{1,0:T(1,128)} %param.19) | copy-start | bytes 30724
  9.2 68.3 %copy-start.2 = (s32[4]{0:T(128)S(1)}, s32[4]{0:T(128)}, u32[]{:S(2)}) copy-start(s32[4]{0:T(128)} %param.18) | copy-start | bytes 52
  77.5 71.5 %reduce-scatter.6.cloned.1.call-start = ((), (), s32[]{:S(2)}) async-start(), calls=%async_computation.4 | async-start | bytes 819200 | tf_op jit(solution)/shard_map/while
  109.7 9.8 %copy-start = (bf16[1,2560,640]{2,1,0:T(8,128)(2,1)S(1)}, bf16[1,2560,640]{2,1,0:T(8,128)(2,1)}, u32[]{:S(2)}) copy-start(bf16[1,2560,640]{2,1,0:T(8,128)(2,1)} %get-tuple-element.398) | copy-start | bytes 9830404 | tf_op jit(solution)/shard_map/while/body/eval_jaxpr/cond
  118.2 1.3 copy-start.3
  151.7 6.6 collective-permute-start
  158.3 72.4 %reduce-scatter.6.cloned.1.call-start = ((), (), s32[]{:S(2)}) async-start(), calls=%async_computation.4 | async-start | bytes 819200 | tf_op jit(solution)/shard_map/while
  190.3 9.8 %copy-start = (bf16[1,2560,640]{2,1,0:T(8,128)(2,1)S(1)}, bf16[1,2560,640]{2,1,0:T(8,128)(2,1)}, u32[]{:S(2)}) copy-start(bf16[1,2560,640]{2,1,0:T(8,128)(2,1)} %get-tuple-element.398) | copy-start | bytes 9830404 | tf_op jit(solution)/shard_map/while/body/eval_jaxpr/cond
  233.5 6.7 collective-permute-start
  240.2 73.3 %reduce-scatter.6.cloned.1.call-start = ((), (), s32[]{:S(2)}) async-start(), calls=%async_computation.4 | async-start | bytes 819200 | tf_op jit(solution)/shard_map/while
  272.2 9.8 %copy-start = (bf16[1,2560,640]{2,1,0:T(8,128)(2,1)S(1)}, bf16[1,2560,640]{2,1,0:T(8,128)(2,1)}, u32[]{:S(2)}) copy-start(bf16[1,2560,640]{2,1,0:T(8,128)(2,1)} %get-tuple-element.398) | copy-start | bytes 9830404 | tf_op jit(solution)/shard_map/while/body/eval_jaxpr/cond
  316.2 6.6 collective-permute-start
  322.9 74.2 %reduce-scatter.6.cloned.1.call-start = ((), (), s32[]{:S(2)}) async-start(), calls=%async_computation.4 | async-start | bytes 819200 | tf_op jit(solution)/shard_map/while
  354.9 9.8 %copy-start = (bf16[1,2560,640]{2,1,0:T(8,128)(2,1)S(1)}, bf16[1,2560,640]{2,1,0:T(8,128)(2,1)}, u32[]{:S(2)}) copy-start(bf16[1,2560,640]{2,1,0:T(8,128)(2,1)} %get-tuple-element.398) | copy-start | bytes 9830404 | tf_op jit(solution)/shard_map/while/body/eval_jaxpr/cond
  399.8 6.7 collective-permute-start
  406.4 74.2 %reduce-scatter.6.cloned.1.call-start = ((), (), s32[]{:S(2)}) async-start(), calls=%async_computation.4 | async-start | bytes 819200 | tf_op jit(solution)/shard_map/while
  483.4 6.7 collective-permute-start
  490.1 74.2 %reduce-scatter.6.cloned.1.call-start = ((), (), s32[]{:S(2)}) async-start(), calls=%async_computation.4 | async-start | bytes 819200 | tf_op jit(solution)/shard_map/while
  567.0 6.6 collective-permute-start
  573.7 74.2 %reduce-scatter.6.cloned.1.call-start = ((), (), s32[]{:S(2)}) async-start(), calls=%async_computation.4 | async-start | bytes 819200 | tf_op jit(solution)/shard_map/while
  650.6 6.7 collective-permute-start
  657.3 44.7 %all-reduce.2.cloned.1.call-start = ((), (), s32[]{:S(2)}) async-start(), calls=%async_computation.2 | async-start | bytes 1310720 | tf_op jit(solution)/shard_map/psum | solution.py:20
  658.2 70.5 %all-gather.5.cloned.1.call-start = ((), (), s32[]{:S(2)}) async-start(), calls=%async_computation.3 | async-start | bytes 3276800 | tf_op jit(solution)/shard_map/all_gather | solution.py:207
  (3 other events, 3.8 us)
Sparse Core Ops, SparseCore 0:
  9.6 58.4 all-gather.2
  128.4 20.5 reduce-scatter.5
  209.1 21.6 reduce-scatter.5
  290.9 22.5 reduce-scatter.5
  373.6 23.4 reduce-scatter.5
  433.6 47.0 reduce-scatter.5
  517.2 47.0 reduce-scatter.5
  600.8 47.0 reduce-scatter.5
  660.4 41.5 all-reduce.1
  703.4 25.2 all-gather.4
where the time goes:
time: 740 us; the launch traced here: 737 us
  waiting for transfers between devices  383 us (52%)
  blocking collectives  133 us (18%)
  matrix products  72 us (10%)
  local copies, waits for them, and re-layouts  65.6 us (9%)
  loops' own time  27.8 us (4%)
  starting transfers between devices  23.8 us (3%)
  other arithmetic  19.2 us (3%)
  between operations  13.5 us (2%)
    while x14, waiting for transfers between devices  231 us
    psum x7, blocking collectives, compute(): summed_codes = lax.psum(part_codes, 'tensor')  83.2 us
    all_gather x1, waiting for transfers between devices, shards(): entire = lax.all_gather(inputs, ('section', 'tensor'), axis=3, tiled=True)  58.9 us
    all_gather x7, blocking collectives, advance(): complete_result = lax.all_gather(owned, 'tensor', axis=1, tiled=True)  49.7 us
    psum x1, waiting for transfers between devices, spread(): return lax.psum(jnp.where(mine, array, jnp.zeros_like(array)), axis)  43.7 us
    another operation x1, loops' own time, shards(): arrived, stored = lax.fori_loop(0, step_count, advance, (initial, stored))  27.4 us
    all_gather x1, waiting for transfers between devices, shards(): complete = lax.all_gather(result, 'tensor', axis=2, tiled=True)  26.7 us
    ppermute x7, starting transfers between devices, shifted(): lax.ppermute(value, axis, [(source, source + steps) for source in range(l...  23.7 us
  transfers between devices with their start and end apart: 17, of which 17 were waited for; matrix products, arithmetic and copies ran while one was open for 0% of the time, Pallas kernels for 0%

commit v1 on v0

--- a/solution.py
+++ b/solution.py
@@ -148,7 +148,7 @@
                 jnp.zeros((tok_rows, lowrank_width), jnp.float32),
             ),
         )
-        summed_codes = lax.psum(part_codes, "tensor")
+        summed_codes = jnp.sum(lax.all_gather(part_codes, "tensor"), axis=0)
         column_job = (
             lax.broadcasted_iota(jnp.int32, (lowrank_width,), 0) // ADAPTER_RANK % ADAPTER_JOBS
         )

time: 740 us -> 702 us (0.949)
  blocking collectives: 133 us -> 90.5 us
    psum x7 -> x0, blocking collectives: 83.2 us -> none  [compute(): summed_codes = lax.psum(part_codes, 'tensor')]
    all_gather x0 -> x7, blocking collectives: none -> 40.9 us  [compute(): summed_codes = jnp.sum(lax.all_gather(part_codes, 'tensor'), axis=0)]
where the time goes in v1:
time: 702 us; the launch traced here: 699 us
  waiting for transfers between devices  387 us (55%)
  blocking collectives  90.5 us (13%)
  matrix products  72 us (10%)
  local copies, waits for them, and re-layouts  65.6 us (9%)
  loops' own time  27.8 us (4%)
  starting transfers between devices  23.8 us (3%)
  other arithmetic  19.3 us (3%)
  between operations  13.5 us (2%)
    while x14, waiting for transfers between devices  235 us
    all_gather x1, waiting for transfers between devices, shards(): entire = lax.all_gather(inputs, ('section', 'tensor'), axis=3, tiled=True)  58.9 us
    all_gather x7, blocking collectives, advance(): complete_result = lax.all_gather(owned, 'tensor', axis=1, tiled=True)  49.6 us
    psum x1, waiting for transfers between devices, spread(): return lax.psum(jnp.where(mine, array, jnp.zeros_like(array)), axis)  43.7 us
    all_gather x7, blocking collectives, compute(): summed_codes = jnp.sum(lax.all_gather(part_codes, 'tensor'), axis=0)  40.9 us
    another operation x1, loops' own time, shards(): arrived, stored = lax.fori_loop(0, step_count, advance, (initial, stored))  27.4 us
    all_gather x1, waiting for transfers between devices, shards(): complete = lax.all_gather(result, 'tensor', axis=2, tiled=True)  26.5 us
    ppermute x7, starting transfers between devices, shifted(): lax.ppermute(value, axis, [(source, source + steps) for source in range(l...  23.7 us
  transfers between devices with their start and end apart: 17, of which 17 were waited for; matrix products, arithmetic and copies ran while one was open for 0% of the time, Pallas kernels for 0%

profile of v1, /device:TPU:0, one launch (start us, length us, event | category | flops | bytes accessed | tf_op | source)
XLA Modules:
  0.0 699.3 jit_solution(8982303179844730280)
XLA Ops:
  9.2 58.9 %all-gather.6.cloned.1.call-done = bf16[4,2,64,2560]{2,0,1,3:T(4,128)(2,1)} async-done(((bf16[4,2,64,160]{2,0,1,3:T(4,128)(2,1)}), bf16[4,2,64,2560]{2,0,1,3:T(4,128)(2,1)}) %all-gather.6.cloned.1.call-update) | async-done | bytes 2621456 | tf_op jit(solution)/shard_map/all_gather | solution.py:124
  68.1 8.5 %copy.28 = bf16[4,2,64,2560]{3,2,1,0:T(8,128)(2,1)} copy(bf16[4,2,64,2560]{2,0,1,3:T(4,128)(2,1)} %all-gather.6.cloned.1.call-done) | data formatting | bytes 5242880 | tf_op jit(solution)/shard_map/while | solution.py:205
  77.5 541.9 %while.17 = (s32[]{:T(128)}, bf16[128,640]{1,0:T(8,128)(2,1)S(1)}, bf16[4,128,640]{2,1,0:T(8,128)(2,1)}, pred[]{:T(512)}, s32[4]{0:T(128)S(1)}, /*index=5*/bf16[...) while((s32[]{:T(128)}, bf16[128,640]{1,0:T(8,128)(2,1)S(1)}, ...), condition=%wide.region_10.11_spmd, body=%wide.region_0.10_spmd.sunk | while | flops 1744780416 | bytes 45433628 | solution.py:205
  82.6 7.9 %all_gather.39 = bf16[128,2560]{1,0:T(8,128)(2,1)S(1)} all-gather(bf16[128,640]{1,0:T(8,128)(2,1)S(1)} %dynamic-slice_select_fusion.2), channel_id=1, replica_groups=mesh['section'=4,'dp'=2,'tensor'=4] {'tensor'}, dimensions={1}, use_global_device_ids=true | all-gather | bytes 819200 | tf_op jit(solution)/shard_map/while/body/eval_jaxpr/all_gather | solution.py:194
  93.0 5.9 all-gather.2
  99.8 22.1 %conditional.5 = (bf16[128,2560]{1,0:T(8,128)(2,1)S(1)}) conditional(s32[]{:T(128)} %convert_element_type.120, () %tuple.63, (bf16[1,2560,640]{2,1,0:T(8,128)(2,1)}, bf16[128,2560]{1,0:T(8,128)(2,1)}, bf16[128,128]{1,0:T(8,128)(2,1)S(1)}, bf16[1,2,64,640]{3,2,1,0:T(8,128)(2,1)}, bf16[1,2560,640]{2,1,0:T(8,128)(2,1)}, ...), branch_computations={%region_5.5_spmd, %region_6.8_spmd} | conditional | flops 1720939136 | bytes 34157632 | solution.py:158
  123.0 19.8 %reduce-scatter.6.cloned.1.call-done = bf16[640,128]{1,0:T(8,128)(2,1)} async-done(((bf16[2560,128]{1,0:T(8,128)(2,1)}), bf16[640,128]{1,0:T(8,128)(2,1)}) %reduce-scatter.6.cloned.1.call-update) | async-done | bytes 163856 | tf_op jit(solution)/shard_map/while
  157.2 7.0 all_gather.39
  173.5 22.1 %conditional.5 = (bf16[128,2560]{1,0:T(8,128)(2,1)S(1)}) conditional(s32[]{:T(128)} %convert_element_type.120, () %tuple.63, (bf16[1,2560,640]{2,1,0:T(8,128)(2,1)}, bf16[128,2560]{1,0:T(8,128)(2,1)}, bf16[128,128]{1,0:T(8,128)(2,1)S(1)}, bf16[1,2,64,640]{3,2,1,0:T(8,128)(2,1)}, bf16[1,2560,640]{2,1,0:T(8,128)(2,1)}, ...), branch_computations={%region_5.5_spmd, %region_6.8_spmd} | conditional | flops 1720939136 | bytes 34157632 | solution.py:158
  196.7 22.6 %reduce-scatter.6.cloned.1.call-done = bf16[640,128]{1,0:T(8,128)(2,1)} async-done(((bf16[2560,128]{1,0:T(8,128)(2,1)}), bf16[640,128]{1,0:T(8,128)(2,1)}) %reduce-scatter.6.cloned.1.call-update) | async-done | bytes 163856 | tf_op jit(solution)/shard_map/while
  233.7 6.9 all_gather.39
  250.0 22.1 %conditional.5 = (bf16[128,2560]{1,0:T(8,128)(2,1)S(1)}) conditional(s32[]{:T(128)} %convert_element_type.120, () %tuple.63, (bf16[1,2560,640]{2,1,0:T(8,128)(2,1)}, bf16[128,2560]{1,0:T(8,128)(2,1)}, bf16[128,128]{1,0:T(8,128)(2,1)S(1)}, bf16[1,2,64,640]{3,2,1,0:T(8,128)(2,1)}, bf16[1,2560,640]{2,1,0:T(8,128)(2,1)}, ...), branch_computations={%region_5.5_spmd, %region_6.8_spmd} | conditional | flops 1720939136 | bytes 34157632 | solution.py:158
  273.2 23.6 %reduce-scatter.6.cloned.1.call-done = bf16[640,128]{1,0:T(8,128)(2,1)} async-done(((bf16[2560,128]{1,0:T(8,128)(2,1)}), bf16[640,128]{1,0:T(8,128)(2,1)}) %reduce-scatter.6.cloned.1.call-update) | async-done | bytes 163856 | tf_op jit(solution)/shard_map/while
  311.1 7.0 all_gather.39
  327.4 22.1 %conditional.5 = (bf16[128,2560]{1,0:T(8,128)(2,1)S(1)}) conditional(s32[]{:T(128)} %convert_element_type.120, () %tuple.63, (bf16[1,2560,640]{2,1,0:T(8,128)(2,1)}, bf16[128,2560]{1,0:T(8,128)(2,1)}, bf16[128,128]{1,0:T(8,128)(2,1)S(1)}, bf16[1,2,64,640]{3,2,1,0:T(8,128)(2,1)}, bf16[1,2560,640]{2,1,0:T(8,128)(2,1)}, ...), branch_computations={%region_5.5_spmd, %region_6.8_spmd} | conditional | flops 1720939136 | bytes 34157632 | solution.py:158
  350.6 24.5 %reduce-scatter.6.cloned.1.call-done = bf16[640,128]{1,0:T(8,128)(2,1)} async-done(((bf16[2560,128]{1,0:T(8,128)(2,1)}), bf16[640,128]{1,0:T(8,128)(2,1)}) %reduce-scatter.6.cloned.1.call-update) | async-done | bytes 163856 | tf_op jit(solution)/shard_map/while
  389.4 7.0 all_gather.39
  405.3 48.1 %reduce-scatter.6.cloned.1.call-done = bf16[640,128]{1,0:T(8,128)(2,1)} async-done(((bf16[2560,128]{1,0:T(8,128)(2,1)}), bf16[640,128]{1,0:T(8,128)(2,1)}) %reduce-scatter.6.cloned.1.call-update) | async-done | bytes 163856 | tf_op jit(solution)/shard_map/while
  467.8 6.9 all_gather.39
  483.6 48.1 %reduce-scatter.6.cloned.1.call-done = bf16[640,128]{1,0:T(8,128)(2,1)} async-done(((bf16[2560,128]{1,0:T(8,128)(2,1)}), bf16[640,128]{1,0:T(8,128)(2,1)}) %reduce-scatter.6.cloned.1.call-update) | async-done | bytes 163856 | tf_op jit(solution)/shard_map/while
  546.1 6.9 all_gather.39
  561.9 48.1 %reduce-scatter.6.cloned.1.call-done = bf16[640,128]{1,0:T(8,128)(2,1)} async-done(((bf16[2560,128]{1,0:T(8,128)(2,1)}), bf16[640,128]{1,0:T(8,128)(2,1)}) %reduce-scatter.6.cloned.1.call-update) | async-done | bytes 163856 | tf_op jit(solution)/shard_map/while
  620.4 43.7 %all-reduce.2.cloned.1.call-done = bf16[4,128,640]{2,1,0:T(8,128)(2,1)} async-done(((bf16[4,128,640]{2,1,0:T(8,128)(2,1)}), bf16[4,128,640]{2,1,0:T(8,128)(2,1)}) %all-reduce.2.cloned.1.call-update) | async-done | bytes 655376 | tf_op jit(solution)/shard_map/psum | solution.py:20
  664.1 26.5 %all-gather.8.cloned.1.call-done = bf16[4,128,2560]{2,1,0:T(8,128)(2,1)} async-done(((bf16[4,128,640]{2,1,0:T(8,128)(2,1)}), bf16[4,128,2560]{2,1,0:T(8,128)(2,1)}) %all-gather.8.cloned.1.call-update) | async-done | bytes 2621456 | tf_op jit(solution)/shard_map/all_gather | solution.py:207
  (245 shorter events, 243.3 us)
Async XLA Ops:
  6.5 61.6 %all-gather.6.cloned.1.call-start = ((), (), s32[]{:S(2)}) async-start(), calls=%async_computation.1 | async-start | bytes 5570560 | tf_op jit(solution)/shard_map/all_gather | solution.py:124
  9.2 68.3 %copy-start.1 = (f32[1,2560]{1,0:T(1,128)S(1)}, f32[1,2560]{1,0:T(1,128)}, u32[]{:S(2)}) copy-start(f32[1,2560]{1,0:T(1,128)} %param.19) | copy-start | bytes 30724
  9.2 68.3 %copy-start.2 = (s32[4]{0:T(128)S(1)}, s32[4]{0:T(128)}, u32[]{:S(2)}) copy-start(s32[4]{0:T(128)} %param.18) | copy-start | bytes 52
  77.5 65.3 %reduce-scatter.6.cloned.1.call-start = ((), (), s32[]{:S(2)}) async-start(), calls=%async_computation.4 | async-start | bytes 819200 | tf_op jit(solution)/shard_map/while
  104.4 9.8 %copy-start = (bf16[1,2560,640]{2,1,0:T(8,128)(2,1)S(1)}, bf16[1,2560,640]{2,1,0:T(8,128)(2,1)}, u32[]{:S(2)}) copy-start(bf16[1,2560,640]{2,1,0:T(8,128)(2,1)} %get-tuple-element.398) | copy-start | bytes 9830404 | tf_op jit(solution)/shard_map/while/body/eval_jaxpr/cond
  113.0 1.3 copy-start.3
  145.5 6.6 collective-permute-start
  152.2 67.1 %reduce-scatter.6.cloned.1.call-start = ((), (), s32[]{:S(2)}) async-start(), calls=%async_computation.4 | async-start | bytes 819200 | tf_op jit(solution)/shard_map/while
  178.0 9.8 %copy-start = (bf16[1,2560,640]{2,1,0:T(8,128)(2,1)S(1)}, bf16[1,2560,640]{2,1,0:T(8,128)(2,1)}, u32[]{:S(2)}) copy-start(bf16[1,2560,640]{2,1,0:T(8,128)(2,1)} %get-tuple-element.398) | copy-start | bytes 9830404 | tf_op jit(solution)/shard_map/while/body/eval_jaxpr/cond
  222.0 6.7 collective-permute-start
  228.7 68.0 %reduce-scatter.6.cloned.1.call-start = ((), (), s32[]{:S(2)}) async-start(), calls=%async_computation.4 | async-start | bytes 819200 | tf_op jit(solution)/shard_map/while
  254.5 9.8 %copy-start = (bf16[1,2560,640]{2,1,0:T(8,128)(2,1)S(1)}, bf16[1,2560,640]{2,1,0:T(8,128)(2,1)}, u32[]{:S(2)}) copy-start(bf16[1,2560,640]{2,1,0:T(8,128)(2,1)} %get-tuple-element.398) | copy-start | bytes 9830404 | tf_op jit(solution)/shard_map/while/body/eval_jaxpr/cond
  299.4 6.6 collective-permute-start
  306.1 69.0 %reduce-scatter.6.cloned.1.call-start = ((), (), s32[]{:S(2)}) async-start(), calls=%async_computation.4 | async-start | bytes 819200 | tf_op jit(solution)/shard_map/while
  332.0 9.8 %copy-start = (bf16[1,2560,640]{2,1,0:T(8,128)(2,1)S(1)}, bf16[1,2560,640]{2,1,0:T(8,128)(2,1)}, u32[]{:S(2)}) copy-start(bf16[1,2560,640]{2,1,0:T(8,128)(2,1)} %get-tuple-element.398) | copy-start | bytes 9830404 | tf_op jit(solution)/shard_map/while/body/eval_jaxpr/cond
  377.7 6.7 collective-permute-start
  384.4 68.9 %reduce-scatter.6.cloned.1.call-start = ((), (), s32[]{:S(2)}) async-start(), calls=%async_computation.4 | async-start | bytes 819200 | tf_op jit(solution)/shard_map/while
  456.1 6.7 collective-permute-start
  462.7 69.0 %reduce-scatter.6.cloned.1.call-start = ((), (), s32[]{:S(2)}) async-start(), calls=%async_computation.4 | async-start | bytes 819200 | tf_op jit(solution)/shard_map/while
  534.4 6.7 collective-permute-start
  541.1 68.9 %reduce-scatter.6.cloned.1.call-start = ((), (), s32[]{:S(2)}) async-start(), calls=%async_computation.4 | async-start | bytes 819200 | tf_op jit(solution)/shard_map/while
  612.7 6.7 collective-permute-start
  619.4 44.7 %all-reduce.2.cloned.1.call-start = ((), (), s32[]{:S(2)}) async-start(), calls=%async_computation.2 | async-start | bytes 1310720 | tf_op jit(solution)/shard_map/psum | solution.py:20
  620.4 70.3 %all-gather.8.cloned.1.call-start = ((), (), s32[]{:S(2)}) async-start(), calls=%async_computation.3 | async-start | bytes 3276800 | tf_op jit(solution)/shard_map/all_gather | solution.py:207
  (3 other events, 3.8 us)
Sparse Core Ops, SparseCore 0:
  9.6 58.4 all-gather.5
  123.1 19.6 reduce-scatter.5
  196.8 22.4 reduce-scatter.5
  273.3 23.4 reduce-scatter.5
  350.7 24.2 reduce-scatter.5
  405.4 47.9 reduce-scatter.5
  483.7 47.9 reduce-scatter.5
  562.0 47.9 reduce-scatter.5
  622.6 41.5 all-reduce.1
  665.5 25.0 all-gather.7
